TPU v7x, 128 devices: a whole 4x4x4 slice. The times are simulated.
128 devices in a mesh: fsdp: 16 (over y_hi, z, core), tensor: 8 (over y_lo, x).
Axes of the slice: x: 4, y: 4 (y_hi: 2, y_lo: 2; y = y_hi * 2 + y_lo), z: 4, core: 2. Of those that a mesh axis runs over, the one named last changes fastest.
Arguments:
- states: bfloat16 [4096, 8192], P('fsdp'), may hold values from -64 to 64
- segment_ids: int32 [16, 256], P('fsdp'), may hold values from 0 to 3, never falling along the last dimension, each value on 1 to 128 neighbouring positions
- attn_gain: float32 [8192], replicated, may hold values from 0.1 to 1.9
- query_weight: bfloat16 [8192, 4096], P('fsdp', 'tensor'), may hold values from -2 to 2
- key_weight: bfloat16 [8192, 1024], P('fsdp', 'tensor'), may hold values from -2 to 2
- value_matrix: bfloat16 [8192, 1024], P('fsdp', 'tensor'), may hold values from -0.0625 to 0.0625
- out_weight: bfloat16 [4096, 8192], P('tensor', 'fsdp'), may hold values from -0.28125 to 0.28125
- final_gain: float32 [8192], P('tensor'), may hold values from 0.1 to 1.9
- head_weight: float32 [8192], P('tensor'), may hold values from -0.0625 to 0.0625
Outputs:
- scores: float32 [4096], P(('fsdp', 'tensor'))
- resid_out: bfloat16 [4096, 8192], P('fsdp', 'tensor')
Inputs may be any that keep to these rules, and one draw needn't show every extreme that they name: `segment_ids`: in each row, segment numbers never fall and each rollout spans 1 to 128 positions.
All inputs are finite; a program needn't handle non-finite values.
Results may differ from a plain program's by a relative error of at most 0.0071.
Values may be sent and summed in bfloat16 or wider, within the bound.
A program may use at most 128 MiB of HBM per device.

v0:
```python
import jax
import jax.numpy as jnp
from jax import lax
from jax.sharding import PartitionSpec as P

MODEL_WIDTH = 8192
HEAD_SIZE = 128


EPS = 1e-05
THETA = 500000.0
NEG_FILL = -1e30


def in_one_piece(arrays, axis, dim, along):
    both = jnp.concatenate(arrays, axis=along)
    result, at, outs = (lax.all_gather(both, axis, axis=dim, tiled=True), 0, [])
    for a in arrays:
        outs.append(lax.slice_in_dim(result, at, at + a.shape[along], axis=along))
        at += a.shape[along]
    return tuple(outs)


def sent_to_all(value, axis):
    length = lax.axis_size(axis)
    return lax.all_to_all(
        jnp.broadcast_to(value[None], (length, *value.shape)), axis, 0, 0, tiled=True
    )


def over_copies(value, axis):
    return sent_to_all(value, axis).sum(axis=0)


def together(arrays, axis):
    ravelled, at, outs = (jnp.concatenate([a.reshape(-1) for a in arrays]), 0, [])
    total = over_copies(ravelled, axis)
    for a in arrays:
        outs.append(total[at : at + a.size].reshape(a.shape))
        at += a.size
    return tuple(outs)


def rope_tables(seg_row):
    count = seg_row.shape[0]
    places = jnp.arange(count, dtype=jnp.int32)
    boundary = jnp.concatenate([jnp.ones((1,), dtype=bool), seg_row[1:] != seg_row[:-1]])
    begins = lax.cummax(jnp.where(boundary, places, jnp.zeros_like(places)), axis=0)
    positions = (places - begins).astype(jnp.float32)
    half_width = HEAD_SIZE // 2
    frequency = THETA ** (-(2.0 * jnp.arange(half_width, dtype=jnp.float32)) / HEAD_SIZE)
    angles = positions[:, None] * frequency[None, :]
    return (jnp.cos(angles), jnp.sin(angles))


def rotated(block, cosine, sine_part):
    half_width = block.shape[-1] // 2
    first_half = block[..., :half_width]
    second_half = block[..., half_width:]
    cos_rows = cosine[:, None, :]
    sin_rows = sine_part[:, None, :]
    return jnp.concatenate(
        [
            first_half * cos_rows - second_half * sin_rows,
            second_half * cos_rows + first_half * sin_rows,
        ],
        axis=-1,
    )


def attend(queries, key_rows, values, seg_row):
    t_rows = queries.shape[0]
    heads_here = queries.shape[1] // HEAD_SIZE
    groups_here = key_rows.shape[1] // HEAD_SIZE
    ratio = heads_here // groups_here
    cosine, sine_part = rope_tables(seg_row)
    query_rot = rotated(queries.reshape(t_rows, heads_here, HEAD_SIZE), cosine, sine_part).astype(
        jnp.bfloat16
    )
    key_rot = rotated(key_rows.reshape(t_rows, groups_here, HEAD_SIZE), cosine, sine_part).astype(
        jnp.bfloat16
    )
    value_rows = values.astype(jnp.bfloat16).reshape(t_rows, groups_here, HEAD_SIZE)
    grouped = query_rot.reshape(t_rows, groups_here, ratio, HEAD_SIZE)
    logits = jnp.einsum(
        "tkgd,skd->kgts", grouped, key_rot, preferred_element_type=jnp.float32
    ) * HEAD_SIZE ** (-0.5)
    places = jnp.arange(t_rows, dtype=jnp.int32)
    allowed = (seg_row[:, None] == seg_row[None, :]) & (places[None, :] <= places[:, None])
    logits = jnp.where(allowed[None, None], logits, NEG_FILL)
    row_peak = jnp.max(logits, axis=-1, keepdims=True)
    raised = jnp.exp(logits - row_peak)
    probabilities = (raised / jnp.sum(raised, axis=-1, keepdims=True)).astype(jnp.bfloat16)
    mixed = jnp.einsum(
        "kgts,skd->tkgd", probabilities, value_rows, preferred_element_type=jnp.float32
    )
    return mixed.astype(jnp.bfloat16).reshape(t_rows, heads_here * HEAD_SIZE)


def body(
    states,
    segment_ids,
    attn_gain,
    query_weight,
    key_weight,
    value_matrix,
    out_weight,
    final_gain,
    head_weight,
):
    t_rows, width = states.shape
    tensor_count = lax.axis_size("tensor")
    tensor_index = lax.axis_index("tensor")
    widened = states.astype(jnp.float32)
    normed = (
        widened
        * lax.rsqrt(jnp.sum(widened * widened, axis=1, keepdims=True) / MODEL_WIDTH + EPS)
        * attn_gain[None, :]
    ).astype(jnp.bfloat16)

    def add_piece(portion):
        return jnp.dot(normed, portion, preferred_element_type=jnp.float32)

    pieces = in_one_piece((query_weight, key_weight, value_matrix), "fsdp", 0, 1)
    queries = add_piece(pieces[0])
    key_rows = add_piece(pieces[1])
    values = add_piece(pieces[2])
    mixed = attend(queries, key_rows, values, segment_ids[0])
    slice_cols = width // tensor_count
    partials = jnp.dot(
        mixed,
        lax.all_gather(out_weight, "fsdp", axis=1, tiled=True),
        preferred_element_type=jnp.float32,
    )
    branch = lax.psum_scatter(partials, "tensor", scatter_dimension=1, tiled=True)
    own_cols = lax.dynamic_slice_in_dim(widened, tensor_index * slice_cols, slice_cols, 1)
    resid_out = (own_cols + branch).astype(jnp.bfloat16)
    stream = resid_out.astype(jnp.float32)
    squares = jnp.sum(stream * stream, axis=1)
    products = jnp.sum(stream * (final_gain * head_weight)[None, :], axis=1)
    share_rows = t_rows // tensor_count
    squares_all, products_all = together((squares, products), "tensor")
    local_squares = lax.dynamic_slice_in_dim(squares_all, tensor_index * share_rows, share_rows, 0)
    products_mine = lax.dynamic_slice_in_dim(products_all, tensor_index * share_rows, share_rows, 0)
    scores = products_mine * lax.rsqrt(local_squares / MODEL_WIDTH + EPS)
    return (scores, resid_out)


def solution(mesh):
    placed = (
        P("fsdp", None),
        P("fsdp", None),
        P(),
        P("fsdp", "tensor"),
        P("fsdp", "tensor"),
        P("fsdp", "tensor"),
        P("tensor", "fsdp"),
        P("tensor"),
        P("tensor"),
    )
    return jax.shard_map(
        body,
        mesh=mesh,
        in_specs=placed,
        out_specs=(P(("fsdp", "tensor")), P("fsdp", "tensor")),
        check_vma=False,
    )
```

profile of v0, /device:TPU:13, one launch (start us, length us, event | category | flops | bytes accessed | tf_op | source)
XLA Modules:
  0.0 295.1 jit_solution(9830881361931489665)
XLA Ops:
  7.2 0.0 all-gather.3.cloned.1.call-start
  7.2 2.1 pad_maximum_fusion
  9.3 0.0 all-gather.3.cloned.1.call-update
  9.4 0.0 all-gather.5.cloned.1.call-start
  9.4 0.7 all-gather.5.cloned.1.call-update
  10.1 0.0 reduce-scatter.2.cloned.1.call-start
  10.2 0.8 compare_reduce_fusion
  11.0 0.1 fusion.40
  11.1 0.3 reduce-window.9
  11.4 0.1 slice.47
  11.5 0.1 slice_reduce_fusion
  11.6 3.1 %multiply_reduce_fusion = f32[256]{0:T(256)S(1)} fusion(bf16[256,8192]{1,0:T(8,128)(2,1)} %param.9), kind=kLoop, calls=%fused_computation.3 | loop fusion | flops 6291200 | bytes 4195328 | tf_op jit(solution)/shard_map/reduce_sum | solution.py:117
  14.8 0.1 fusion.41
  14.8 0.9 fusion.27
  15.7 0.5 multiply_cosine_fusion
  16.2 0.0 copy-start.2
  16.2 86.6 %all-gather.3.cloned.1.call-done = bf16[8192,768]{1,0:T(8,128)(2,1)} async-done(((bf16[512,768]{1,0:T(8,128)(2,1)}), bf16[8192,768]{1,0:T(8,128)(2,1)}) %all-gather.3.cloned.1.call-update) | async-done | bytes 12582928 | tf_op jit(solution)/shard_map/all_gather | solution.py:17
  102.8 7.0 %fusion = f32[256,512]{1,0:T(8,128)S(1)} fusion(bf16[8192,768]{1,0:T(8,128)(2,1)} %all-gather.3.cloned.1.call-done, f32[8192]{0:T(1024)} %param.11, f32[256]{0:T(256)S(1)} %add_rsqrt_fusion, bf16[256,8192]{1,0:T(8,128)(2,1)} %param.9), kind=kOutput, calls=%fused_computation | convolution fusion | flops 2155872256 | bytes 13140992 | tf_op jit(solution)/shard_map/dot_general | solution.py:122
  109.9 0.2 reshape.251
  110.1 0.0 copy-done.2
  110.1 4.7 %fusion.8 = f32[256,1,128]{0,2,1:T(8,128)S(1)} fusion(bf16[8192,768]{1,0:T(8,128)(2,1)} %all-gather.3.cloned.1.call-done, f32[8192]{0:T(1024)S(1)} %copy-done.2, f32[256]{0:T(256)S(1)} %add_rsqrt_fusion, bf16[256,8192]{1,0:T(8,128)(2,1)} %param.9), kind=kOutput, calls=%fused_computation.14 | convolution fusion | flops 545259520 | bytes 6456320 | tf_op jit(solution)/shard_map/dot_general | solution.py:122
  114.8 0.3 fusion.39
  115.1 0.3 fusion.43
  115.4 0.1 subtract_convert_fusion
  115.6 0.4 fusion.45
  116.0 0.2 fusion.21
  116.2 4.6 %convolution_convert_fusion = bf16[128,4,256]{2,0,1:T(8,128)(2,1)S(1)} fusion(bf16[8192,768]{1,0:T(8,128)(2,1)} %all-gather.3.cloned.1.call-done, f32[1,4,256,256]{2,3,1,0:T(8,128)S(1)} %get-tuple-element.16, f32[4,256]{1,0:T(4,128)S(1)} %fusion.21, f32[4,256]{1,0:T(4,128)S(1)} %get-tuple-element.15, f32[8192]{0:T(1024)S(1)} %copy-done.2, ...), kind=kOutput, calls=%fused_computation.13 | convolution fusion | flops 613318656 | bytes 7644160 | tf_op jit(solution)/shard_map/kgts,skd->tkgd/dot_general | solution.py:94
  120.7 58.6 %all-gather.5.cloned.1.call-done = bf16[512,8192]{1,0:T(8,128)(2,1)} async-done(((bf16[512,512]{1,0:T(8,128)(2,1)}), bf16[512,8192]{1,0:T(8,128)(2,1)}) %all-gather.5.cloned.1.call-update) | async-done | bytes 8388624 | tf_op jit(solution)/shard_map/all_gather | solution.py:132
  179.3 9.0 %fusion.46 = f32[256,8192]{1,0:T(8,128)} fusion(bf16[256,512]{0,1:T(8,128)(2,1)S(1)} %bitcast.40, bf16[512,8192]{1,0:T(8,128)(2,1)} %all-gather.5.cloned.1.call-done), kind=kOutput, calls=%fused_computation.64 | convolution fusion | flops 2147483648 | bytes 17039360 | tf_op jit(solution)/shard_map/dot_general | solution.py:130
  188.3 0.0 reduce-scatter.2.cloned.1.call-update
  188.3 0.0 copy-start
  188.3 0.0 copy-start.1
  188.3 6.4 %convert_element_type.41 = f32[256,8192]{1,0:T(8,128)} convert(bf16[256,8192]{1,0:T(8,128)(2,1)} %param.9) | non-fusion elementwise | flops 2097152 | bytes 12582912 | tf_op jit(solution)/shard_map/convert_element_type | solution.py:114
  194.7 0.0 copy-done
  194.7 0.0 copy-done.1
  194.7 81.7 %reduce-scatter.2.cloned.1.call-done = f32[256,1024]{1,0:T(8,128)} async-done(((f32[256,8192]{1,0:T(8,128)}), f32[256,1024]{1,0:T(8,128)}) %reduce-scatter.2.cloned.1.call-update) | async-done | bytes 1048592 | tf_op jit(solution)/shard_map/reduce_scatter | solution.py:135
  276.5 2.5 fusion.19
  279.0 0.6 broadcast_in_dim.15
  279.6 6.0 %all-to-all-start = ((f32[8,1,512]{2,1,0:T(1,128)}), f32[8,1,512]{2,1,0:T(1,128)S(1)}, u32[]{:S(2)}, u32[]{:S(2)}) async-start(f32[8,1,512]{2,1,0:T(1,128)} %broadcast_in_dim.15), calls=%async_computation.1 | async-start | bytes 32768 | tf_op jit(solution)/shard_map/all_to_all | solution.py:26
  285.6 2.4 all-to-all-done
  288.0 0.6 rsqrt_multiply_fusion
  (7 shorter events, 0.1 us)
Async XLA Ops:
  7.2 95.7 %all-gather.3.cloned.1.call-start = ((), (), s32[]{:S(2)}) async-start(), calls=%async_computation.2 | async-start | bytes 13369344 | tf_op jit(solution)/shard_map/all_gather | solution.py:17
  9.4 169.9 %all-gather.5.cloned.1.call-start = ((), (), s32[]{:S(2)}) async-start(), calls=%async_computation.3 | async-start | bytes 8912896 | tf_op jit(solution)/shard_map/all_gather | solution.py:132
  10.1 266.4 %reduce-scatter.2.cloned.1.call-start = ((), (), s32[]{:S(2)}) async-start(), calls=%async_computation.4 | async-start | bytes 9437184 | tf_op jit(solution)/shard_map/reduce_scatter | solution.py:135
  16.2 93.9 %copy-start.2 = (f32[8192]{0:T(1024)S(1)}, f32[8192]{0:T(1024)}, u32[]{:S(2)}) copy-start(f32[8192]{0:T(1024)} %param.11) | copy-start | bytes 98308
  188.3 6.4 %copy-start = (f32[1024]{0:T(1024)S(1)}, f32[1024]{0:T(1024)}, u32[]{:S(2)}) copy-start(f32[1024]{0:T(1024)} %param.16) | copy-start | bytes 12292
  188.3 6.4 %copy-start.1 = (f32[1024]{0:T(1024)S(1)}, f32[1024]{0:T(1024)}, u32[]{:S(2)}) copy-start(f32[1024]{0:T(1024)} %param.17) | copy-start | bytes 12292
  279.6 8.3 %all-to-all-start = ((f32[8,1,512]{2,1,0:T(1,128)}), f32[8,1,512]{2,1,0:T(1,128)S(1)}, u32[]{:S(2)}, u32[]{:S(2)}) async-start(f32[8,1,512]{2,1,0:T(1,128)} %broadcast_in_dim.15), calls=%async_computation.1 | async-start | bytes 32768 | tf_op jit(solution)/shard_map/all_to_all | solution.py:26
Sparse Core Ops, SparseCore 0:
  10.5 92.3 all-gather.2
  105.1 74.1 all-gather.4
  188.4 88.0 reduce-scatter.1
where the time goes:
time: 299 us; the launch traced here: 295 us
  waiting for transfers between devices  230 us (77%)
  matrix products  25.7 us (9%)
  other arithmetic  18.2 us (6%)
  between operations  13.9 us (5%)
  starting transfers between devices  6.08 us (2%)
    all_gather x1, waiting for transfers between devices, in_one_piece(): result, at, outs = (lax.all_gather(both, axis, axis=dim, tiled=True), 0, [])  86.6 us
    reduce_scatter x1, waiting for transfers between devices, body(): lax.psum_scatter(partials, 'tensor', scatter_dimension=1, tiled=True)  81.7 us
    all_gather x1, waiting for transfers between devices, body(): lax.all_gather(out_weight, 'fsdp', axis=1, tiled=True)  58.6 us
    dot_general x2, matrix products, add_piece(): return jnp.dot(normed, portion, preferred_element_type=jnp.float32)  11.7 us
    dot_general x1, matrix products, body(): jnp.dot(mixed, lax.all_gather(out_weight, 'fsdp', axis=1, tiled=True), pr...  8.98 us
    convert_element_type x1, other arithmetic, body(): widened = states.astype(jnp.float32)  6.4 us
  transfers between devices with their start and end apart: 4, of which 4 were waited for; matrix products, arithmetic and copies ran while one was open for 10% of the time, Pallas kernels for 0%

commit v1 on v0

v1 whole, which is shorter than its diff:
```python
import functools

import jax
import jax.numpy as jnp
import numpy as np
from jax import lax
from jax.experimental import pallas as pl
from jax.experimental.pallas import tpu as pltpu
from jax.sharding import PartitionSpec as P

WIDTH = 8192
HEAD = 128
HEADS_HERE = 4
TOK = 256
EPS = 1e-05
THETA = 500000.0
NEG_FILL = -1e30
MESH = pl.DeviceIdType.MESH
F32 = jnp.float32
BF16 = jnp.bfloat16

ORIGINS = ((0, 0), (0, -1), (0, 1), (1, 0), (0, 2), (1, -1), (1, 1), (1, 2))
ROWS = 512
SPLIT_QKV = 288
SPLIT_OUT = 384
KINDS = ("x", "x", "x", "x", "x", "x", "x", "x")
N_SEM = 160


def kernel(
    states_hbm, seg_ref, gain_ref, q_hbm, k_hbm, v_hbm, o_hbm, fg_ref, hw_ref, freq_ref,
    scores_ref, resid_ref,
    st, normed, wqkv, wout, acc, mixed, part, xin, yin, ssum, res, fgs, hws,
    lsem, ssem, rsem,
):
    f = lax.axis_index("fsdp")
    t = lax.axis_index("tensor")
    core = lax.rem(f, 2)
    zz = lax.rem(f // 2, 4)
    yh = f // 8
    yl = t // 4
    xx = lax.rem(t, 4)

    def fdev(dy, dz, other_core=False):
        y2 = 1 - yh if dy else yh
        z2 = lax.rem(zz + dz + 4, 4)
        c2 = 1 - core if other_core else core
        return (y2 * 4 + z2) * 2 + c2

    def pair_of(origin):
        y2 = 1 - yh if origin[0] else yh
        return y2 * 4 + lax.rem(zz + origin[1] + 4, 4)

    zp, zm, ypart, sib = (fdev(0, 1), t), (fdev(0, -1), t), (fdev(1, 0), t), (fdev(0, 0, True), t)
    xpeer = [(f, yl * 4 + lax.rem(xx + d, 4)) for d in (1, 2, 3)]
    tpeer = [(f, lax.rem(t + d, 8)) for d in range(1, 8)]

    barrier = pltpu.get_barrier_semaphore()
    peers = [zp, zm, ypart, sib] + tpeer
    for d in peers:
        pl.semaphore_signal(barrier, inc=1, device_id=d, device_id_type=MESH)

    own_q = pltpu.make_async_copy(q_hbm, wqkv.at[f // 2, pl.ds(core * ROWS, ROWS), pl.ds(0, 512)], lsem.at[0])
    own_k = pltpu.make_async_copy(k_hbm, wqkv.at[f // 2, pl.ds(core * ROWS, ROWS), pl.ds(512, 128)], lsem.at[1])
    own_v = pltpu.make_async_copy(v_hbm, wqkv.at[f // 2, pl.ds(core * ROWS, ROWS), pl.ds(640, 128)], lsem.at[2])
    own_s = pltpu.make_async_copy(states_hbm, st, lsem.at[3])
    own_o = pltpu.make_async_copy(o_hbm, wout.at[f // 2, core], lsem.at[4])
    for cp in (own_q, own_k, own_v, own_s, own_o):
        cp.start()

    ids = {}

    def sem_id(name):
        return ids.setdefault(name, len(ids))

    sent = []

    def send(src, dst, device, name):
        i = sem_id(name)
        cp = pltpu.make_async_remote_copy(
            src_ref=src, dst_ref=dst, send_sem=ssem.at[i], recv_sem=rsem.at[i],
            device_id=device, device_id_type=MESH,
        )
        cp.start()
        sent.append(cp)

    def arrived(dst, name):
        i = sem_id(name)
        pltpu.make_async_remote_copy(
            src_ref=dst, dst_ref=dst, send_sem=ssem.at[i], recv_sem=rsem.at[i],
            device_id=zp, device_id_type=MESH,
        ).wait_recv()

    class Gather:
        def __init__(self, tag, split):
            self.tag = tag
            h = split // 2
            g = (ROWS - split) // 2
            self.span = {
                "1": (0, split), "1A": (0, h), "1B": (h, split - h),
                "2": (split, ROWS - split), "2A": (split, g), "2B": (split + g, ROWS - split - g),
                "all": (0, ROWS),
            }

        def at(self, origin, piece, mine=True):
            lo, n = self.span[piece]
            c = core if mine else 1 - core
            if self.tag == "q":
                return wqkv.at[pair_of(origin), pl.ds(pl.multiple_of(c * ROWS + lo, 16), n), :]
            return wout.at[pair_of(origin), c, pl.ds(lo, n), :]

        def name(self, origin, piece):
            return (self.tag, origin, piece)

        def send(self, origin, piece, device, seen_as):
            ref = self.at(origin, piece)
            send(ref, ref, device, self.name(seen_as, piece))

        def wait(self, origin, piece):
            arrived(self.at(origin, piece), self.name(origin, piece))

        def cross(self, origin):
            ref = self.at(origin, "all")
            send(ref, ref, sib, (self.tag, origin, "sib"))

        def wait_cross(self, origin):
            arrived(self.at(origin, "all", mine=False), (self.tag, origin, "sib"))

        def s0(self):
            o = (0, 0)
            self.send(o, "1", ypart, (1, 0))
            self.send(o, "1", zp, (0, -1))
            self.send(o, "1", zm, (0, 1))
            self.send(o, "2", zp, (0, -1))
            self.send(o, "2", zm, (0, 1))
            self.send(o, "2", ypart, (1, 0))
            self.cross(o)

        def s1(self):
            self.wait((1, 0), "1")
            self.send((1, 0), "1", zp, (1, -1))
            self.send((1, 0), "1", zm, (1, 1))

        def s2(self):
            self.wait((0, -1), "2")
            self.send((0, -1), "2A", zp, (0, 2))
            self.send((0, -1), "2", ypart, (1, -1))
            self.wait((0, 1), "2")
            self.send((0, 1), "2B", zm, (0, 2))
            self.send((0, 1), "2", ypart, (1, 1))

        def s3(self):
            self.wait((0, -1), "1")
            self.send((0, -1), "1A", zp, (0, 2))
            self.wait((0, 1), "1")
            self.send((0, 1), "1B", zm, (0, 2))
            self.cross((0, -1))
            self.cross((0, 1))
            self.wait((1, 0), "2")
            self.cross((1, 0))

        def s4(self):
            self.wait((1, -1), "1")
            self.send((1, -1), "1A", zp, (1, 2))
            self.wait((1, 1), "1")
            self.send((1, 1), "1B", zm, (1, 2))

        def s5(self):
            self.wait((0, 2), "2A")
            self.send((0, 2), "2A", ypart, (1, 2))
            self.wait((0, 2), "2B")
            self.send((0, 2), "2B", ypart, (1, 2))

        def s6(self):
            self.wait((0, 2), "1A")
            self.wait((0, 2), "1B")
            self.cross((0, 2))

        def s7(self):
            self.wait((1, -1), "2")
            self.cross((1, -1))
            self.wait((1, 1), "2")
            self.cross((1, 1))

        def s8(self):
            for piece in ("1A", "1B", "2A", "2B"):
                self.wait((1, 2), piece)
            self.cross((1, 2))

    gq = Gather("q", SPLIT_QKV)
    go = Gather("o", SPLIT_OUT)

    own_q.wait()
    own_k.wait()
    own_v.wait()
    pl.semaphore_wait(barrier, len(peers))
    gq.s0()
    for n, d in enumerate(tpeer):
        send(fg_ref, fgs.at[t], d, ("fg", n))
        send(hw_ref, hws.at[t], d, ("hw", n))
    fgs[t] = fg_ref[...]
    hws[t] = hw_ref[...]

    own_s.wait()
    acc[...] = jnp.zeros_like(acc)

    @pl.loop(0, TOK // 32)
    def _(rb):
        rows = pl.ds(pl.multiple_of(rb * 32, 32), 32)
        total = jnp.zeros((32, 128), F32)
        for cb in range(WIDTH // 512):
            v = st[rows, cb * 512:(cb + 1) * 512].astype(F32)
            v = v * v
            total += v[:, :128] + v[:, 128:256] + v[:, 256:384] + v[:, 384:]
        scale = lax.rsqrt(jnp.sum(total, axis=1, keepdims=True) / WIDTH + EPS)
        for cb in range(WIDTH // 512):
            v = st[rows, cb * 512:(cb + 1) * 512].astype(F32)
            g = gain_ref[:, cb * 512:(cb + 1) * 512]
            normed[rows, cb * 512:(cb + 1) * 512] = (v * scale * g).astype(BF16)

    def project(origin):
        gq.wait_cross(origin)
        p = pair_of(origin)
        cols = pl.ds(pl.multiple_of(p * 1024, 1024), 1024)
        acc[...] += jnp.dot(normed[:, cols], wqkv[p], preferred_element_type=F32)

    project((0, 0))

    seg_row = seg_ref[...].astype(F32)
    row_i = lax.broadcasted_iota(jnp.int32, (TOK, TOK), 0)
    col_i = lax.broadcasted_iota(jnp.int32, (TOK, TOK), 1)
    seg_all = jnp.broadcast_to(seg_row, (TOK, TOK))
    seg_col = jnp.sum(jnp.where(row_i == col_i, seg_all, 0.0), axis=1, keepdims=True)
    same = seg_all == seg_col
    first = jnp.min(jnp.where(same, col_i.astype(F32), 1e9), axis=1, keepdims=True)
    position = lax.broadcasted_iota(jnp.int32, (TOK, 1), 0).astype(F32) - first
    allowed = same & (col_i <= row_i)
    angle = position * freq_ref[...]
    cos2 = jnp.cos(angle)
    sin2 = jnp.sin(angle)
    lane = lax.broadcasted_iota(jnp.int32, (TOK, HEAD), 1)
    sin2 = jnp.where(lane < HEAD // 2, -sin2, sin2)

    gq.s1()
    gq.s2()
    gq.s3()
    project((0, -1))
    project((0, 1))
    project((1, 0))
    gq.s4()
    gq.s5()
    own_o.wait()
    go.s0()
    gq.s6()
    gq.s7()
    project((0, 2))
    project((1, -1))
    project((1, 1))
    gq.s8()
    project((1, 2))

    def rotate(block):
        return (block * cos2 + pltpu.roll(block, HEAD // 2, 1) * sin2).astype(BF16)

    key_rot = rotate(acc[:, 512:640])
    value_rows = acc[:, 640:768].astype(BF16)
    for h in range(HEADS_HERE):
        query_rot = rotate(acc[:, h * HEAD:(h + 1) * HEAD])
        logits = lax.dot_general(
            query_rot, key_rot, (((1,), (1,)), ((), ())), preferred_element_type=F32
        ) * HEAD ** (-0.5)
        logits = jnp.where(allowed, logits, NEG_FILL)
        raised = jnp.exp(logits - jnp.max(logits, axis=1, keepdims=True))
        probs = (raised / jnp.sum(raised, axis=1, keepdims=True)).astype(BF16)
        out = jnp.dot(probs, value_rows, preferred_element_type=F32)
        mixed[:, h * HEAD:(h + 1) * HEAD] = out.astype(BF16)

    sums = [jnp.zeros((32, 128), F32), jnp.zeros((32, 128), F32)]

    def expand(n):
        origin = ORIGINS[n]
        go.wait_cross(origin)
        p = pair_of(origin)
        for j in range(2):
            block = jnp.dot(mixed[...], wout[p, j], preferred_element_type=F32)
            part[n, :, :, :, j * 512:(j + 1) * 512] = block.astype(BF16).reshape(2, 4, 32, 512)
        if KINDS[n] == "x":
            for d in range(3):
                send(part.at[n, :, xpeer[d][1] - yl * 4], xin.at[n, d], xpeer[d], ("rs1", n, d))
        else:
            send(part.at[n, 1 - yl], yin.at[n], (f, (1 - yl) * 4 + xx), ("rs1", n))

    def middle(n):
        if KINDS[n] == "x":
            total = part[n, :, xx].astype(F32)
            for d in range(3):
                arrived(xin.at[n, d], ("rs1", n, d))
                total += xin[n, d].astype(F32)
            ssum[n, 0:2] = total.astype(BF16)
            send(ssum.at[n, 1 - yl], yin.at[n, 0], (f, (1 - yl) * 4 + xx), ("rs2", n))
        else:
            arrived(yin.at[n], ("rs1", n))
            ssum[n] = (part[n, yl].astype(F32) + yin[n].astype(F32)).astype(BF16)
            for d in range(3):
                send(ssum.at[n, xpeer[d][1] - yl * 4], xin.at[n, d, 0], xpeer[d], ("rs2", n, d))

    res_sends = []

    def finish(n):
        p = pair_of(ORIGINS[n])
        if KINDS[n] == "x":
            arrived(yin.at[n, 0], ("rs2", n))
            total = ssum[n, yl].astype(F32) + yin[n, 0].astype(F32)
        else:
            total = ssum[n, xx].astype(F32)
            for d in range(3):
                arrived(xin.at[n, d, 0], ("rs2", n, d))
                total += xin[n, d, 0].astype(F32)
        cols = pl.ds(pl.multiple_of(p * 1024, 1024), 1024)
        mine = st[pl.ds(pl.multiple_of(t * 32, 32), 32), cols].astype(F32)
        out = (mine + total).astype(BF16)
        res[n] = out
        stream = out.astype(F32)
        gh = fgs[p] * hws[p]
        sq = stream * stream
        pr = stream * gh
        for b in range(8):
            sums[0] += sq[:, b * 128:(b + 1) * 128]
            sums[1] += pr[:, b * 128:(b + 1) * 128]
        i = sem_id(("res", n))
        cp = pltpu.make_async_remote_copy(
            src_ref=res.at[n], dst_ref=resid_ref.at[pl.ds(pl.multiple_of(t * 32, 32), 32), :],
            send_sem=ssem.at[i], recv_sem=rsem.at[N_SEM + t],
            device_id=(f, p), device_id_type=MESH,
        )
        res_sends.append((p, cp))

        @pl.when(p != t)
        def _():
            cp.start()

        @pl.when(p == t)
        def _():
            resid_ref[pl.ds(pl.multiple_of(t * 32, 32), 32), :] = out

    for n, d in enumerate(tpeer):
        src = lax.rem(t + 8 - (n + 1), 8)
        arrived(fgs.at[src], ("fg", n))
        arrived(hws.at[src], ("hw", n))

    expand(0)
    go.s1()
    go.s2()
    go.s3()
    expand(1)
    expand(2)
    go.s4()
    go.s5()
    expand(3)
    middle(0)
    go.s6()
    expand(4)
    middle(1)
    go.s7()
    expand(5)
    expand(6)
    middle(2)
    go.s8()
    expand(7)
    finish(0)
    middle(3)
    finish(1)
    middle(4)
    finish(2)
    middle(5)
    finish(3)
    middle(6)
    finish(4)
    middle(7)
    finish(5)
    finish(6)
    finish(7)

    squares = jnp.sum(sums[0], axis=1, keepdims=True)
    products = jnp.sum(sums[1], axis=1, keepdims=True)
    scores_ref[...] = products * lax.rsqrt(squares / WIDTH + EPS)

    for d in range(1, 8):
        src = lax.rem(t + d, 8)
        rows = resid_ref.at[pl.ds(pl.multiple_of(src * 32, 32), 32), :]
        pltpu.make_async_remote_copy(
            src_ref=rows, dst_ref=rows, send_sem=ssem.at[0], recv_sem=rsem.at[N_SEM + src],
            device_id=zp, device_id_type=MESH,
        ).wait_recv()
    for cp in sent:
        cp.wait_send()
    for p, cp in res_sends:
        @pl.when(p != t)
        def _():
            cp.wait_send()
    assert len(ids) <= N_SEM, len(ids)


def body(states, segment_ids, attn_gain, query_weight, key_weight, value_matrix, out_weight,
         final_gain, head_weight):
    half = HEAD // 2
    freq = THETA ** (-(2.0 * jnp.arange(half, dtype=F32)) / HEAD)
    freq = jnp.concatenate([freq, freq]).reshape(1, HEAD)
    hbm = pl.BlockSpec(memory_space=pl.ANY)
    vmem = pl.BlockSpec(memory_space=pltpu.VMEM)
    n = len(ORIGINS)
    scores, resid = pl.pallas_call(
        kernel,
        out_shape=(
            jax.ShapeDtypeStruct((32, 1), F32),
            jax.ShapeDtypeStruct((TOK, 1024), BF16),
        ),
        in_specs=[hbm, vmem, vmem, hbm, hbm, hbm, hbm, vmem, vmem, vmem],
        out_specs=(vmem, vmem),
        scratch_shapes=[
            pltpu.VMEM((TOK, WIDTH), BF16),
            pltpu.VMEM((TOK, WIDTH), BF16),
            pltpu.VMEM((8, 1024, 768), BF16),
            pltpu.VMEM((8, 2, 512, 512), BF16),
            pltpu.VMEM((TOK, 768), F32),
            pltpu.VMEM((TOK, 512), BF16),
            pltpu.VMEM((n, 2, 4, 32, 1024), BF16),
            pltpu.VMEM((n, 3, 2, 32, 1024), BF16),
            pltpu.VMEM((n, 4, 32, 1024), BF16),
            pltpu.VMEM((n, 4, 32, 1024), BF16),
            pltpu.VMEM((n, 32, 1024), BF16),
            pltpu.VMEM((8, 1, 1024), F32),
            pltpu.VMEM((8, 1, 1024), F32),
            pltpu.SemaphoreType.DMA((5,)),
            pltpu.SemaphoreType.DMA((N_SEM,)),
            pltpu.SemaphoreType.DMA((N_SEM + 8,)),
        ],
        compiler_params=pltpu.CompilerParams(
            collective_id=0, has_side_effects=True, vmem_limit_bytes=62 * 1024 * 1024
        ),
        name="critic",
    )(
        states, segment_ids, attn_gain.reshape(1, WIDTH), query_weight, key_weight, value_matrix,
        out_weight, final_gain.reshape(1, 1024), head_weight.reshape(1, 1024), freq,
    )
    return scores.reshape(32), resid


def solution(mesh):
    placed = (
        P("fsdp", None), P("fsdp", None), P(), P("fsdp", "tensor"), P("fsdp", "tensor"),
        P("fsdp", "tensor"), P("tensor", "fsdp"), P("tensor"), P("tensor"),
    )
    return jax.shard_map(
        body, mesh=mesh, in_specs=placed,
        out_specs=(P(("fsdp", "tensor")), P("fsdp", "tensor")), check_vma=False,
    )
```

time: 299 us -> 125 us (0.42); the launches traced: 295 us -> 124 us
  waiting for transfers between devices: 230 us -> 0 us
  Pallas kernels: 0 us -> 120 us
  matrix products: 25.7 us -> 0 us
  other arithmetic: 18.2 us -> 1.95 us
  between operations: 13.9 us -> 0.64 us
  starting transfers between devices: 6.08 us -> 0 us
    all_gather x2 -> x0, waiting for transfers between devices: 145 us -> none  [the longest x1 86.6 us: in_one_piece(): result, at, outs = (lax.all_gather(both, axis, axis=dim, tiled=True), 0, [])]
    pallas_call x0 -> x1, Pallas kernels: none -> 120 us  [body(): pl.pallas_call(kernel, out_shape=(jax.ShapeDtypeStruct((32, 1), F32), jax...]
    reduce_scatter x1 -> x0, waiting for transfers between devices: 81.7 us -> none  [body(): lax.psum_scatter(partials, 'tensor', scatter_dimension=1, tiled=True)]
    dot_general x5 -> x0, matrix products: 25.7 us -> none  [the longest x2 11.7 us: add_piece(): return jnp.dot(normed, portion, preferred_element_type=jnp.float32)]
    convert_element_type x2 -> x0, other arithmetic: 6.47 us -> none  [the longest x1 6.4 us: body(): widened = states.astype(jnp.float32)]
    all_to_all x1 -> x0, starting transfers between devices: 5.96 us -> none  [sent_to_all(): lax.all_to_all(jnp.broadcast_to(value[None], (length, *value.shape)), axi...]
    reduce_sum x4 -> x0, other arithmetic: 5.83 us -> none  [the longest x1 3.11 us: body(): jnp.sum(widened * widened, axis=1, keepdims=True) / MODEL_WIDTH + EPS]
  transfers between devices with their start and end apart: 4 -> 0, of which waited for: 4 -> 0; matrix products, arithmetic and copies ran while one was open for 10% -> 0% of each run, Pallas kernels for 0% -> 0%
where the time goes in v1:
time: 125 us; the launch traced here: 124 us
  Pallas kernels  120 us (96%)
  other arithmetic  1.95 us (2%)
  local copies, waits for them, and re-layouts  1.87 us (1%)
    pallas_call x1, Pallas kernels, body(): pl.pallas_call(kernel, out_shape=(jax.ShapeDtypeStruct((32, 1), F32), jax...  120 us

profile of v1, /device:TPU:13, one launch (start us, length us, event | category | flops | bytes accessed | tf_op | source)
XLA Modules:
  0.0 124.4 jit_solution(6162213658658554196)
XLA Ops:
  0.6 0.6 maximum_bitcast_fusion.freq_ref
  1.2 119.9 %critic.1 = (f32[32,1]{1,0:T(8,128)}, bf16[256,1024]{1,0:T(8,128)(2,1)}) custom-call(bf16[256,8192]{1,0:T(8,128)(2,1)} %states_hbm.1, s32[1,256]{1,0:T(1,128)} %seg_ref.1, f32[1,8192]{1,0:T(1,128)} %bitcast.5, bf16[512,512]{1,0:T(8,128)(2,1)} %q_hbm.1, bf16[512,128]{1,0:T(8,128)(2,1)} %k_hbm.1, bf16[512,128]{1,0:T(8,128)(2,1)} %v_hbm.1, ...), custom_call_target="tpu_custom_call" | custom-call | tf_op jit(solution)/shard_map/critic/pallas_call | solution.py:412
  121.1 1.3 %reduce = f32[32]{0:T(128)} reduce(f32[32,1]{1,0:T(8,128)} %get-tuple-element.4, f32[]{:T(128)} %constant.8), dimensions={1}, to_apply=%get-tuple-element.4.reduce_sub_computation | reduce | bytes 260 | tf_op jit(solution)/shard_map/critic/pallas_call | solution.py:412
  122.5 1.9 %copy.12 = bf16[256,1024]{1,0:T(8,128)(2,1)} copy(bf16[256,1024]{1,0:T(8,128)(2,1)} %get-tuple-element.9) | data formatting | bytes 1048576
  (1 shorter events, 0.0 us)
